TPU v7x, 128 devices: a whole 4x4x4 slice. The times are simulated.
128 devices in a mesh: rows: 32 (over z, y, core), cols: 4 (over x).
Axes of the slice: x: 4, y: 4, z: 4, core: 2. Of those that a mesh axis runs over, the one named last changes fastest.
Arguments:
- w_gate: float32 [2048, 8192], P('rows', 'cols'), may hold values from -0.25 to 0.25
- first_gate: float32 [2048, 8192], P('rows', 'cols'), may hold values from -6 to 6
- second_gate: float32 [2048, 8192], P('rows', 'cols'), may hold values from 0.1 to 10
- w_up: float32 [2048, 8192], P('rows', 'cols'), may hold values from -0.25 to 0.25
- first_up: float32 [2048, 8192], P('rows', 'cols'), may hold values from -6 to 6
- second_up: float32 [2048, 8192], P('rows', 'cols'), may hold values from 0.1 to 10
- norm_train: float32 [2048], P(('rows', 'cols')), may hold values from 0.25 to 1.75
- norm_step: float32 [2048], P(('rows', 'cols')), may hold values from -0.3 to 0.3
Outputs:
- ready_gate: bfloat16 [2048, 8192], P(None, 'cols')
- ready_up: bfloat16 [2048, 8192], P(None, 'cols')
- column_gate: float32 [8192], P('cols')
- column_up: float32 [8192], P('cols')
- serve_norm: bfloat16 [2048], replicated
- latest_gate: float32 [2048, 8192], P('rows', 'cols')
- latest_up: float32 [2048, 8192], P('rows', 'cols')
All inputs are finite; a program needn't handle non-finite values. Where the computation divides by a largest or mean magnitude, that divisor is 1e-20 or more.
Results may differ from a plain program's by a relative error of at most 0.001.
Values may be sent and summed in bfloat16 or wider, within the bound.
A program may use at most 128 MiB of HBM per device.

v0:
```python
import jax
import jax.numpy as jnp
from jax import lax
from jax.sharding import Mesh
from jax.sharding import PartitionSpec as P

D_MODEL = 2048
ROWS = ("rows_0", "rows_1", "rows_2")
ROWS_COLS = ("rows_0", "rows_1", "rows_2", "cols")


learn_rate = 0.01
decay_rate = 0.1
tiny_value = 1e-08


def from_everyone(value, axis):
    length = lax.axis_size(axis)
    return lax.all_to_all(
        jnp.broadcast_to(value[None], (length, *value.shape)), axis, 0, 0, tiled=True
    )


def of_everyone(value, axis):
    return from_everyone(value, axis).sum(axis=0)


def together(arrays, axis):
    ends = [0]
    for a in arrays:
        ends.append(ends[-1] + a.size)
    so_far = of_everyone(jnp.concatenate([a.ravel() for a in arrays]), axis)
    return tuple((so_far[b:e].reshape(a.shape) for a, b, e in zip(arrays, ends, ends[1:])))


def sent_together(arrays, axis, dim, along):
    ends, at = ([], 0)
    for a in arrays[:-1]:
        at += a.shape[along]
        ends.append(at)
    both = jnp.concatenate(arrays, axis=along)
    return tuple(jnp.split(lax.all_gather(both, axis, axis=dim, tiled=True), ends, axis=along))


def joined_along(pieces, dim):
    lengths = list(pieces.shape[1:])
    lengths[dim] *= pieces.shape[0]
    return jnp.moveaxis(pieces, 0, dim).reshape(lengths)


def stacked_from(value, axes, order):
    pieces = value[None]
    for k in order:
        pieces = lax.all_gather(pieces, axes[k], axis=0, tiled=True)
    current = [lax.axis_size(axes[k]) for k in reversed(order)]
    pieces = pieces.reshape(*current, *value.shape)
    turned = sorted(range(len(order)), key=lambda place: order[len(order) - 1 - place])
    return pieces.transpose(*turned, *range(len(order), pieces.ndim)).reshape(-1, *value.shape)


def gather_axes(value, axes, order, dim):
    return joined_along(stacked_from(value, axes, order), dim)


def local(w_gate, first_gate, second_gate, w_up, first_up, second_up, norm_train, norm_step):
    latest_gate = w_gate - learn_rate * (
        first_gate / (jnp.sqrt(second_gate) + tiny_value) + decay_rate * w_gate
    )
    latest_up = w_up - learn_rate * (
        first_up / (jnp.sqrt(second_up) + tiny_value) + decay_rate * w_up
    )
    total_gate, total_up = together(
        (jnp.sum(jnp.abs(latest_gate), axis=0), jnp.sum(jnp.abs(latest_up), axis=0)), ROWS
    )
    column_gate = total_gate / D_MODEL
    column_up = total_up / D_MODEL
    narrow_gate, narrow_up = (
        (latest_gate / column_gate).astype(jnp.bfloat16),
        (latest_up / column_up).astype(jnp.bfloat16),
    )
    ready_gate, ready_up = sent_together((narrow_gate, narrow_up), ROWS, 0, 1)
    serve_norm = gather_axes(
        (norm_train + norm_step).astype(jnp.bfloat16), ROWS_COLS, (0, 1, 3, 2), 0
    )
    return (ready_gate, ready_up, column_gate, column_up, serve_norm, latest_gate, latest_up)


def solution(mesh):
    torus = Mesh(
        mesh.devices.reshape(4, 4, 2, mesh.shape["cols"]), ("rows_0", "rows_1", "rows_2", "cols")
    )
    in_specs = (
        P(ROWS, "cols"),
        P(ROWS, "cols"),
        P(ROWS, "cols"),
        P(ROWS, "cols"),
        P(ROWS, "cols"),
        P(ROWS, "cols"),
        P(ROWS_COLS),
        P(ROWS_COLS),
    )
    out_specs = (
        P(None, "cols"),
        P(None, "cols"),
        P("cols"),
        P("cols"),
        P(),
        P(ROWS, "cols"),
        P(ROWS, "cols"),
    )
    return jax.shard_map(local, mesh=torus, in_specs=in_specs, out_specs=out_specs, check_vma=False)
```

profile of v0, /device:TPU:1, one launch (start us, length us, event | category | flops | bytes accessed | tf_op | source)
XLA Modules:
  0.0 121.9 jit_solution(6254912166650149929)
XLA Ops:
  7.2 0.0 copy-start.6
  7.2 0.0 copy-start.4
  7.2 0.0 copy-start.5
  7.2 0.0 all-gather.5.cloned.1.call-start
  7.2 2.4 %abs_reduce_fusion = (f32[2048]{0:T(1024)S(1)}, f32[64,2048]{1,0:T(8,128)S(1)}, f32[2048]{0:T(1024)S(1)}, f32[64,2048]{1,0:T(8,128)S(1)}) fusion(f32[64,2048]{1,0:T(8,128)} %param.11, f32[64,2048]{1,0:T(8,128)} %param.12, f32[64,2048]{1,0:T(8,128)} %param.13, f32[64,2048]{1,0:T(8,128)} %param.8, f32[64,2048]{1,0:T(8,128)} %param.9, f32[64,2048]{1,0:T(8,128)} %param.10), kind=kLoop, calls=%fused_computation.3 | loop fusion | flops 2093056 | bytes 4210688 | tf_op jit(solution)/shard_map/reduce_sum | solution.py:73
  9.7 0.0 copy-start
  9.7 0.0 copy-start.1
  9.7 0.5 broadcast_in_dim.4
  10.2 20.8 %all_to_all.6 = f32[32,1,4096]{2,1,0:T(1,128)S(1)} all-to-all(f32[32,1,4096]{2,1,0:T(1,128)S(1)} %broadcast_in_dim.4), channel_id=1, replica_groups=mesh['rows_0'=4,'rows_1'=4,'rows_2'=2,'cols'=4] {'rows_0','rows_1','rows..., dimensions={0} | all-to-all | bytes 1048576 | tf_op jit(solution)/shard_map/all_to_all | solution.py:19
  31.0 0.4 reduce_sum.29
  31.4 0.0 copy-start.2
  31.4 0.0 copy-start.3
  31.5 0.8 pad_maximum_fusion
  32.3 0.0 all-gather.5.cloned.1.call-update
  32.3 0.0 copy-done.6
  32.4 0.6 dynamic-slice
  33.6 0.0 copy-done.4
  33.6 0.0 copy-done.5
  33.6 0.2 dynamic-update-slice
  33.9 6.8 %all-reduce = bf16[64]{0:T(256)(128)(2,1)S(1)} all-reduce(bf16[64]{0:T(256)(128)(2,1)S(1)} %dynamic-update-slice), channel_id=2, replica_groups=mesh['rows_0'=4,'rows_1'=4,'rows_2'=2,'cols'=4] {'rows_0'}, use_global_device_ids=true, to_apply=%add | all-reduce | flops 64 | bytes 256
  40.7 0.1 reshape.30
  40.8 7.7 %all-gather.1 = bf16[4,4,16]{2,1,0:T(4,128)(2,1)S(1)} all-gather(bf16[1,4,16]{2,1,0:T(4,128)(2,1)S(1)} %reshape.30), channel_id=1, replica_groups=mesh['rows_0'=4,'rows_1'=4,'rows_2'=2,'cols'=4] {'rows_1'}, dimensions={0}, use_global_device_ids=true | all-gather | bytes 640 | tf_op jit(solution)/shard_map/all_gather | solution.py:54
  48.5 9.8 %all_gather.18 = bf16[64,16]{1,0:T(8,128)(2,1)S(1)} all-gather(bf16[16,16]{1,0:T(8,128)(2,1)S(1)} %bitcast.8), channel_id=1, replica_groups=mesh['rows_0'=4,'rows_1'=4,'rows_2'=2,'cols'=4] {'cols'}, dimensions={0}, use_global_device_ids=true | all-gather | bytes 2560 | tf_op jit(solution)/shard_map/all_gather | solution.py:54
  58.4 0.1 copy.26
  58.5 6.4 %all-gather.2 = bf16[2,64,16]{1,2,0:T(8,128)(2,1)S(1)} all-gather(bf16[1,64,16]{1,2,0:T(8,128)(2,1)S(1)} %copy.26), channel_id=1, replica_groups=mesh['rows_0'=4,'rows_1'=4,'rows_2'=2,'cols'=4] {'rows_2'}, dimensions={0}, use_global_device_ids=true | all-gather | bytes 6144 | tf_op jit(solution)/shard_map/all_gather | solution.py:54
  64.9 0.1 copy.27
  65.0 0.7 reshape_reshape.3
  65.7 37.4 %all-gather.5.cloned.1.call-done = bf16[2048,4096]{1,0:T(8,128)(2,1)} async-done(((bf16[64,4096]{1,0:T(8,128)(2,1)}), bf16[2048,4096]{1,0:T(8,128)(2,1)}) %all-gather.5.cloned.1.call-update) | async-done | bytes 16777232 | tf_op jit(solution)/shard_map/all_gather | solution.py:42
  103.1 11.9 %fusion = (bf16[2048,2048]{1,0:T(8,128)(2,1)}, bf16[2048,2048]{1,0:T(8,128)(2,1)}) fusion(bf16[2048,4096]{1,0:T(8,128)(2,1)} %all-gather.5.cloned.1.call-done), kind=kLoop, calls=%fused_computation.11 | loop fusion | bytes 33554432 | tf_op jit(solution)/shard_map/split | solution.py:42
  115.0 0.0 copy-done
  115.0 0.0 copy-done.1
  115.0 0.0 copy-done.2
  (8 shorter events, 0.1 us)
Async XLA Ops:
  7.2 25.2 %copy-start.6 = (u32[128]{0:T(128)S(1)}, u32[128]{0:T(128)}, u32[]{:S(2)}) copy-start(u32[128]{0:T(128)} %constant.16) | copy-start | bytes 1540
  7.2 26.4 %copy-start.4 = (f32[16]{0:T(128)S(1)}, f32[16]{0:T(128)}, u32[]{:S(2)}) copy-start(f32[16]{0:T(128)} %param.14) | copy-start | bytes 196
  7.2 26.4 %copy-start.5 = (f32[16]{0:T(128)S(1)}, f32[16]{0:T(128)}, u32[]{:S(2)}) copy-start(f32[16]{0:T(128)} %param.15) | copy-start | bytes 196
  7.2 95.9 %all-gather.5.cloned.1.call-start = ((), (), s32[]{:S(2)}) async-start(), calls=%async_computation.1 | async-start | bytes 17301504 | tf_op jit(solution)/shard_map/all_gather | solution.py:42
  9.7 105.4 %copy-start = (f32[64,2048]{1,0:T(8,128)}, f32[64,2048]{1,0:T(8,128)S(1)}, u32[]{:S(2)}) copy-start(f32[64,2048]{1,0:T(8,128)S(1)} %get-tuple-element.10) | copy-start | bytes 1572868
  9.7 105.4 %copy-start.1 = (f32[64,2048]{1,0:T(8,128)}, f32[64,2048]{1,0:T(8,128)S(1)}, u32[]{:S(2)}) copy-start(f32[64,2048]{1,0:T(8,128)S(1)} %get-tuple-element.16) | copy-start | bytes 1572868
  31.4 83.7 %copy-start.2 = (f32[2048]{0:T(1024)}, f32[2048]{0:T(1024)S(1)}, u32[]{:S(2)}) copy-start(f32[2048]{0:T(1024)S(1)} %get-tuple-element.13) | copy-start | bytes 24580
  31.4 83.7 %copy-start.3 = (f32[2048]{0:T(1024)}, f32[2048]{0:T(1024)S(1)}, u32[]{:S(2)}) copy-start(f32[2048]{0:T(1024)S(1)} %get-tuple-element.14) | copy-start | bytes 24580
Sparse Core Ops, SparseCore 0:
  32.5 70.5 all-gather.4
where the time goes:
time: 122 us
  blocking collectives  51.6 us (42%)
  waiting for transfers between devices  37.4 us (31%)
  between operations  14.9 us (12%)
  local copies, waits for them, and re-layouts  14.3 us (12%)
  other arithmetic  3.7 us (3%)
    all_gather x1, waiting for transfers between devices, sent_together(): lax.all_gather(both, axis, axis=dim, tiled=True)  37.4 us
    all_gather x3, blocking collectives, stacked_from(): pieces = lax.all_gather(pieces, axes[k], axis=0, tiled=True)  24 us
    all_to_all x1, blocking collectives, from_everyone(): lax.all_to_all(jnp.broadcast_to(value[None], (length, *value.shape)), axi...  20.8 us
    split x1, local copies, waits for them, and re-layouts, sent_together(): jnp.split(lax.all_gather(both, axis, axis=dim, tiled=True), ends, axis=al...  11.9 us
    unnamed x1, blocking collectives  6.83 us
  transfers between devices with their start and end apart: 1, of which 1 were waited for; matrix products, arithmetic and copies ran while one was open for 1% of the time, Pallas kernels for 0%

commit v1 on v0

v1 whole, which is shorter than its diff:
```python
import heapq

import jax
import jax.numpy as jnp
from jax import lax
from jax.experimental import pallas as pl
from jax.experimental.pallas import tpu as pltpu
from jax.sharding import PartitionSpec as P

D_MODEL = 2048
WIDTH = 2048
ROWS = 64
SIDE = 4
MESH = pl.DeviceIdType.MESH

learn_rate = 0.01
decay_rate = 0.1
tiny_value = 1e-08

PIECE = 32
CHUNKS = tuple((mat, off) for off in range(0, ROWS, PIECE) for mat in range(2))
LOW = tuple(range(len(CHUNKS) // 2))
HIGH = tuple(range(len(CHUNKS) // 2, len(CHUNKS)))


def follow_ups(da, db, c):
    if (da, db) == (0, 0):
        return ("A+", "A-", "B+", "B-")
    if db == 0:
        on = ("B+", "B-")
        if da == 3 and c in LOW:
            on = ("A+",) + on
        if da == 1 and c in HIGH:
            on = ("A-",) + on
        return on
    if db == 3 and c in LOW:
        return ("B+",)
    if db == 1 and c in HIGH:
        return ("B-",)
    return ()


def seen_by_receiver(link, da, db):
    step = -1 if link[1] == "+" else 1
    return ((da + step) % 4, db) if link[0] == "A" else (da, (db + step) % 4)


def arrival_order():
    unit, delay = 1.0, 1.4 * len(CHUNKS) / 4
    queues = {k: [] for k in ("A+", "A-", "B+", "B-")}
    done = {k: 0.0 for k in queues}
    events = [(0.0, c, (0, 0, c)) for c in range(len(CHUNKS))]
    order, now, serial = [], 0.0, len(CHUNKS)
    while events or any(queues.values()):
        rate = {}
        for k in queues:
            if queues[k]:
                other = ("B" if k[0] == "A" else "A") + k[1]
                rate[k] = (0.5 if queues[other] else 1.0) / unit
        steps = [(1 - done[k]) / rate[k] for k in rate]
        if events:
            steps.append(events[0][0] - now)
        dt = max(0.0, min(steps))
        now += dt
        for k in rate:
            done[k] += rate[k] * dt
            if done[k] >= 1 - 1e-9:
                da, db, c = queues[k].pop(0)
                done[k] = 0.0
                serial += 1
                heapq.heappush(events, (now + delay, serial, seen_by_receiver(k, da, db) + (c,)))
        while events and events[0][0] <= now + 1e-9:
            item = heapq.heappop(events)[2]
            order.append(item)
            for k in follow_ups(*item):
                queues[k].append(item)
    return order


ORDER = arrival_order()


def gather_kernel(
    w_g, f_g, s_g, w_u, f_u, s_u, norm_in,
    out_g, out_u, col_g, col_u, norm_out, latest_g, latest_u,
    first, second, part, pair, inverse, slots, nslots,
    load_sem, send_sem, recv_sem, die_send, die_recv, sum_send, sum_recv, n_send, n_recv,
):
    row = lax.axis_index("rows")
    x = lax.axis_index("cols")
    core = row % 2
    y = (row // 2) % 4
    z = row // 8
    a = y * (1 - core) + z * core
    b = z * (1 - core) + y * core
    stride_a = 2 + 6 * core
    stride_b = 8 - 6 * core
    partner = row + 1 - 2 * core
    outs = (out_g, out_u)

    def at_a(pos):
        return row + ((pos % 4) - a) * stride_a

    def at_b(pos):
        return row + ((pos % 4) - b) * stride_b

    def at_y(pos):
        return row + ((pos % 4) - y) * 2

    def at_z(pos):
        return row + ((pos % 4) - z) * 8

    latest = (latest_g, latest_u)
    loads = []
    for m, (w, f, s) in enumerate(((w_g, f_g, s_g), (w_u, f_u, s_u))):
        for j, (src, dst) in enumerate(((w, latest[m]), (f, first.at[m]), (s, second.at[m]))):
            copy = pltpu.make_async_copy(src, dst, load_sem.at[3 * m + j])
            copy.start()
            loads.append(copy)

    barrier = pltpu.get_barrier_semaphore()
    peers = [(partner, x)]
    for d in range(1, 4):
        peers += [(at_y(y + d), x), (at_z(z + d), x), (row, (x + d) % 4)]
    for peer in peers:
        pl.semaphore_signal(barrier, inc=1, device_id=peer, device_id_type=MESH)

    for m in range(2):
        for copy in loads[3 * m : 3 * m + 3]:
            copy.wait()

        def step(i, acc, m=m):
            at = pl.ds(pl.multiple_of(i * 8, 8), 8)
            w = latest[m][at, :]
            new = w - learn_rate * (
                first[m, at, :] / (jnp.sqrt(second[m, at, :]) + tiny_value) + decay_rate * w
            )
            latest[m][at, :] = new
            return acc + jnp.abs(new)

        acc = lax.fori_loop(0, ROWS // 8, step, jnp.zeros((8, WIDTH), jnp.float32))
        part[m] = jnp.sum(acc, axis=0, keepdims=True)

    pl.semaphore_wait(barrier, len(peers))

    def remote(src, dst, send, recv, device):
        return pltpu.make_async_remote_copy(
            src_ref=src, dst_ref=dst, send_sem=send, recv_sem=recv,
            device_id=device, device_id_type=MESH,
        )

    sent = []

    def start(copy):
        copy.start()
        sent.append(copy)

    both = remote(part, pair, sum_send.at[0], sum_recv.at[0], (partner, x))
    start(both)

    def norm_stage(i, device_of, me):
        mine = nslots.at[i, me]
        for d in range(1, 4):
            start(remote(mine, mine, n_send.at[3 * i + d - 1], n_recv.at[3 * i + d - 1],
                         device_of(d)))

    def norm_wait(i, me):
        total = None
        for d in range(1, 4):
            frm = (me + 4 - d) % 4
            remote(nslots.at[i, frm], nslots.at[i, frm], n_send.at[3 * i + d - 1],
                   n_recv.at[3 * i + d - 1], (partner, x)).wait_recv()
        for k in range(4):
            total = nslots[i, k] if total is None else total + nslots[i, k]
        return total

    device = row * 4 + x
    nslots[0, x] = norm_in[...]
    norm_stage(0, lambda d: (row, (x + d) % 4), x)

    both.wait_recv()
    places = ((y, z), (z, y))
    movers = ((at_y, at_z), (at_z, at_y))
    for m in range(2):
        slots[0, m, places[m][0]] = part[m] + pair[m]
    for stage in range(2):
        for d in range(1, 4):
            for m in range(2):
                me = places[m][stage]
                mine = slots.at[stage, m, me]
                k = 1 + (stage * 2 + m) * 3 + d - 1
                start(remote(mine, mine, sum_send.at[k], sum_recv.at[k],
                             (movers[m][stage](me + d), x)))
        for m in range(2):
            me = places[m][stage]
            for d in range(1, 4):
                frm = (me + 4 - d) % 4
                k = 1 + (stage * 2 + m) * 3 + d - 1
                remote(slots.at[stage, m, frm], slots.at[stage, m, frm], sum_send.at[k],
                       sum_recv.at[k], (partner, x)).wait_recv()
            total = slots[stage, m, 0]
            for k in range(1, 4):
                total = total + slots[stage, m, k]
            if stage == 0:
                slots[1, m, places[m][1]] = total
            else:
                column = total * (1.0 / D_MODEL)
                (col_g, col_u)[m][...] = column
                inverse[m] = 1.0 / column

    def block_row(da, db, of_core=None):
        return row + ((a + da) % 4 - a) * stride_a + ((b + db) % 4 - b) * stride_b

    def piece(owner, c):
        mat, off = CHUNKS[c]
        return outs[mat].at[pl.ds(pl.multiple_of(owner * ROWS + off, PIECE), PIECE)]

    n = len(CHUNKS)
    links = {"A+": at_a(a + 1), "A-": at_a(a + 3), "B+": at_b(b + 1), "B-": at_b(b + 3)}
    have = {}
    count = [0]

    def pass_on(da, db, c):
        here = piece(block_row(da, db), c)
        for link in follow_ups(da, db, c):
            ra, rb = seen_by_receiver(link, da, db)
            start(remote(here, here, send_sem.at[count[0]], recv_sem.at[(ra * 4 + rb) * n + c],
                         (links[link], x)))
            count[0] += 1
        mat = CHUNKS[c][0]
        got = have.setdefault((da, db, mat), [])
        got.append(c)
        if len(got) == ROWS // PIECE:
            owner = block_row(da, db)
            block = outs[mat].at[pl.ds(pl.multiple_of(owner * ROWS, ROWS), ROWS)]
            k = (da * 4 + db) * 2 + mat
            start(remote(block, block, die_send.at[k], die_recv.at[k], (partner, x)))

    def make_chunk(c):
        mat, off = CHUNKS[c]
        scale = inverse[mat]
        for i in range(0, PIECE, 16):
            rows = pl.ds(pl.multiple_of(row * ROWS + off + i, 16), 16)
            outs[mat][rows, :] = (latest[mat][off + i : off + i + 16, :] * scale).astype(
                jnp.bfloat16
            )

    norm_at = {8: 0, 16: 1, 24: 2, 32: 3}
    for i, (da, db, c) in enumerate(ORDER):
        if i in norm_at:
            s = norm_at[i]
            if s < 3:
                total = norm_wait(s, (x, y, z)[s])
            if s == 0:
                nslots[1, y] = total
                norm_stage(1, lambda d: (at_y(y + d), x), y)
            elif s == 1:
                nslots[2, z] = total
                norm_stage(2, lambda d: (at_z(z + d), x), z)
            elif s == 2:
                nslots[3, 0] = total
                start(remote(nslots.at[3, 0], nslots.at[3, 1], n_send.at[9], n_recv.at[9],
                             (partner, x)))
            else:
                remote(nslots.at[3, 1], nslots.at[3, 1], n_send.at[9], n_recv.at[9],
                       (partner, x)).wait_recv()
                norm_out[...] = (nslots[3, 0] + nslots[3, 1]).astype(jnp.bfloat16)
        if (da, db) == (0, 0):
            make_chunk(c)
        else:
            here = piece(block_row(da, db), c)
            remote(here, here, send_sem.at[0], recv_sem.at[(da * 4 + db) * n + c],
                   (partner, x)).wait_recv()
        pass_on(da, db, c)

    for pa in range(4):
        for pb in range(4):
            owner = partner + ((b + pa) % 4 - b) * stride_b + ((a + pb) % 4 - a) * stride_a
            for mat in range(2):
                block = outs[mat].at[pl.ds(pl.multiple_of(owner * ROWS, ROWS), ROWS)]
                k = (pa * 4 + pb) * 2 + mat
                remote(block, block, die_send.at[k], die_recv.at[k], (partner, x)).wait_recv()
    for copy in sent:
        copy.wait_send()


N_SENDS = sum(len(follow_ups(*item)) for item in ORDER)


def gather(*args):
    f32, bf16 = jnp.float32, jnp.bfloat16
    dma = pltpu.SemaphoreType.DMA
    anywhere = pl.BlockSpec(memory_space=pl.ANY)
    on_chip = pl.BlockSpec(memory_space=pltpu.VMEM)
    return pl.pallas_call(
        gather_kernel,
        name="gather_kernel",
        out_shape=[
            pltpu.VMEM((D_MODEL, WIDTH), bf16),
            pltpu.VMEM((D_MODEL, WIDTH), bf16),
            pltpu.VMEM((1, WIDTH), f32),
            pltpu.VMEM((1, WIDTH), f32),
            pltpu.VMEM((16, 128), bf16),
            pltpu.VMEM((ROWS, WIDTH), f32),
            pltpu.VMEM((ROWS, WIDTH), f32),
        ],
        in_specs=[anywhere] * 6 + [on_chip],
        out_specs=[on_chip] * 7,
        scratch_shapes=[
            pltpu.VMEM((2, ROWS, WIDTH), f32),
            pltpu.VMEM((2, ROWS, WIDTH), f32),
            pltpu.VMEM((2, 1, WIDTH), f32),
            pltpu.VMEM((2, 1, WIDTH), f32),
            pltpu.VMEM((2, 1, WIDTH), f32),
            pltpu.VMEM((2, 2, 4, 1, WIDTH), f32),
            pltpu.VMEM((4, 4, 16, 128), f32),
            dma((6,)),
            dma((N_SENDS,)),
            dma((16 * len(CHUNKS),)),
            dma((32,)),
            dma((32,)),
            dma((13,)),
            dma((13,)),
            dma((10,)),
            dma((10,)),
        ],
        compiler_params=pltpu.CompilerParams(
            collective_id=0, has_side_effects=True, vmem_limit_bytes=30 * 1024 * 1024
        ),
    )(*(pltpu.with_memory_space_constraint(v, pltpu.HBM) for v in args[:6]), *args[6:])


def write_kernel(*refs):
    k = len(refs) // 2
    srcs, dsts, sem = refs[:k], refs[k : 2 * k], refs[2 * k]
    copies, count = [], 0
    for src, dst in zip(srcs, dsts):
        pieces = 4 if src.shape[0] == D_MODEL else 1
        rows = src.shape[0] // pieces
        for p in range(pieces):
            at = pl.ds(p * rows, rows)
            copies.append(pltpu.make_async_copy(src.at[at], dst.at[at], sem.at[count]))
            count += 1
    for copy in copies:
        copy.start()
    for copy in copies:
        copy.wait()


def write(arrays):
    anywhere = pl.BlockSpec(memory_space=pl.ANY)
    return pl.pallas_call(
        write_kernel,
        name="write_kernel",
        out_shape=[jax.ShapeDtypeStruct(v.shape, v.dtype) for v in arrays],
        in_specs=[anywhere] * len(arrays),
        out_specs=[anywhere] * len(arrays),
        scratch_shapes=[pltpu.SemaphoreType.DMA((16,))],
        compiler_params=pltpu.CompilerParams(vmem_limit_bytes=1024 * 1024),
    )(*arrays)


def local(w_gate, first_gate, second_gate, w_up, first_up, second_up, norm_train, norm_step):
    device = lax.axis_index("rows") * 4 + lax.axis_index("cols")
    gain = jnp.tile(norm_train + norm_step, 128).reshape(16, 128)
    slot = lax.broadcasted_iota(jnp.int32, (16, 128), 0) * 8
    slot = slot + lax.broadcasted_iota(jnp.int32, (16, 128), 1) // 16
    placed = jnp.where(slot == device, gain, 0.0)
    held = gather(w_gate, first_gate, second_gate, w_up, first_up, second_up, placed)
    ready_g, ready_u, col_g, col_u, norm, latest_g, latest_u = write(held)
    return (
        ready_g,
        ready_u,
        col_g.reshape(WIDTH),
        col_u.reshape(WIDTH),
        norm.reshape(D_MODEL),
        latest_g,
        latest_u,
    )


def solution(mesh):
    split = P("rows", "cols")
    return jax.shard_map(
        local,
        mesh=mesh,
        in_specs=(split,) * 6 + (P(("rows", "cols")),) * 2,
        out_specs=(P(None, "cols"),) * 2 + (P("cols"),) * 2 + (P(),) + (split,) * 2,
        check_vma=False,
    )
```

time: 122 us -> 71 us (0.58)
  Pallas kernels: 0 us -> 69.3 us
  blocking collectives: 51.6 us -> 0 us
  waiting for transfers between devices: 37.4 us -> 0 us
  between operations: 14.9 us -> 0.66 us
  local copies, waits for them, and re-layouts: 14.3 us -> 0.08 us
  other arithmetic: 3.7 us -> 0.76 us
    pallas_call x0 -> x2, Pallas kernels: none -> 69.3 us  [the longest x1 63.1 us: gather(): pl.pallas_call(gather_kernel, name='gather_kernel', out_shape=[pltpu.VMEM...]
    all_gather x1 -> x0, waiting for transfers between devices: 37.4 us -> none  [sent_together(): lax.all_gather(both, axis, axis=dim, tiled=True)]
    all_gather x3 -> x0, blocking collectives: 24 us -> none  [stacked_from(): pieces = lax.all_gather(pieces, axes[k], axis=0, tiled=True)]
    all_to_all x1 -> x0, blocking collectives: 20.8 us -> none  [from_everyone(): lax.all_to_all(jnp.broadcast_to(value[None], (length, *value.shape)), axi...]
    split x1 -> x0, local copies, waits for them, and re-layouts: 11.9 us -> none  [sent_together(): jnp.split(lax.all_gather(both, axis, axis=dim, tiled=True), ends, axis=al...]
    unnamed x1 -> x0, blocking collectives: 6.83 us -> none
    reduce_sum x2 -> x0, other arithmetic: 2.76 us -> none  [the longest x1 2.41 us: local(): jnp.sum(jnp.abs(latest_up), axis=0)]
  transfers between devices with their start and end apart: 1 -> 0, of which waited for: 1 -> 0; matrix products, arithmetic and copies ran while one was open for 1% -> 0% of each run, Pallas kernels for 0% -> 0%
where the time goes in v1:
time: 71 us; the launch traced here: 70.8 us
  Pallas kernels  69.3 us (98%)
  other arithmetic  0.76 us (1%)
    pallas_call x1, Pallas kernels, gather(): pl.pallas_call(gather_kernel, name='gather_kernel', out_shape=[pltpu.VMEM...  63.1 us
    pallas_call x1, Pallas kernels, write(): pl.pallas_call(write_kernel, name='write_kernel', out_shape=[jax.ShapeDty...  6.27 us

profile of v1, /device:TPU:1, one launch (start us, length us, event | category | flops | bytes accessed | tf_op | source)
XLA Modules:
  0.0 70.8 jit_solution(15964484280229153603)
XLA Ops:
  0.6 0.7 add.13
  1.3 0.1 tile.11
  1.4 0.1 fusion.norm_in
  1.5 63.1 %gather_kernel.1 = (bf16[2048,2048]{1,0:T(8,128)(2,1)S(1)}, bf16[2048,2048]{1,0:T(8,128)(2,1)S(1)}, f32[1,2048]{1,0:T(1,128)S(1)}, f32[1,2048]{1,0:T(1,128)S(1)}...) custom-call(f32[64,2048]{1,0:T(8,128)} %w_g.1, f32[64,2048]{1,0:T(8,128)} %f_g.1, ...), custom_call_target="tpu_custom_call" | custom-call | tf_op jit(solution)/shard_map/gather_kernel/pallas_call | solution.py:295
  64.6 6.3 %write_kernel.1 = (bf16[2048,2048]{1,0:T(8,128)(2,1)}, bf16[2048,2048]{1,0:T(8,128)(2,1)}, f32[1,2048]{1,0:T(1,128)}, f32[1,2048]{1,0:T(1,128)}, bf16[16,128]{1,...) custom-call(bf16[2048,2048]{1,0:T(8,128)(2,1)S(1)} %get-tuple-element.21.refs_0_, ...), custom_call_target="tpu_custom_call" | custom-call | tf_op jit(solution)/shard_map/write_kernel/pallas_call | solution.py:352
  (4 shorter events, 0.0 us)

commit v2 on v1

v2 whole, which is shorter than its diff:
```python
import heapq

import jax
import jax.numpy as jnp
from jax import lax
from jax.experimental import pallas as pl
from jax.experimental.pallas import tpu as pltpu
from jax.sharding import PartitionSpec as P

D_MODEL = 2048
WIDTH = 2048
ROWS = 64
SIDE = 4
MESH = pl.DeviceIdType.MESH

learn_rate = 0.01
decay_rate = 0.1
tiny_value = 1e-08

CHUNKS = ((0, 0, 32), (1, 0, 32), (0, 32, 32), (1, 32, 32))
N = len(CHUNKS)
RAW = (0,)
LOW = (0, 1)
HIGH = (2, 3)
RAW_ROWS = 8
LINKS = ("A+", "A-", "B+", "B-")
NEIGHBOURS = {"A+": (3, 0), "A-": (1, 0), "B+": (0, 3), "B-": (0, 1)}
FINE_TAIL = 14


def follow_ups(da, db, c):
    if (da, db) == (0, 0):
        return () if c in RAW else LINKS
    if db == 0:
        on = ("B+", "B-")
        if da == 3 and c in LOW:
            on = ("A+",) + on
        if da == 1 and c in HIGH:
            on = ("A-",) + on
        return on
    if db == 3 and c in LOW:
        return ("B+",)
    if db == 1 and c in HIGH:
        return ("B-",)
    return ()


def seen_by_receiver(link, da, db):
    step = -1 if link[1] == "+" else 1
    return ((da + step) % 4, db) if link[0] == "A" else (da, (db + step) % 4)


def arrival_order():
    delay = 1.4
    queues = {k: [] for k in LINKS}
    done = {k: 0.0 for k in queues}
    first = [(0, 0, c) for c in range(N) if c not in RAW]
    first += [NEIGHBOURS[k] + (c,) for c in RAW for k in LINKS]
    first += [(0, 0, c) for c in RAW]
    events = [(0.0, i, item) for i, item in enumerate(first)]
    order, now, serial = [], 0.0, len(first)
    while events or any(queues.values()):
        rate = {}
        for k in queues:
            if queues[k]:
                other = ("B" if k[0] == "A" else "A") + k[1]
                size = CHUNKS[queues[k][0][2]][2] / 32
                rate[k] = (0.5 if queues[other] else 1.0) / size
        steps = [(1 - done[k]) / rate[k] for k in rate]
        if events:
            steps.append(events[0][0] - now)
        dt = max(0.0, min(steps))
        now += dt
        for k in rate:
            done[k] += rate[k] * dt
            if done[k] >= 1 - 1e-9:
                da, db, c = queues[k].pop(0)
                done[k] = 0.0
                serial += 1
                heapq.heappush(events, (now + delay, serial, seen_by_receiver(k, da, db) + (c,)))
        while events and events[0][0] <= now + 1e-9:
            item = heapq.heappop(events)[2]
            order.append(item)
            for k in follow_ups(*item):
                queues[k].append(item)
    return order


def group_of(da, db, c):
    if (da, db) in NEIGHBOURS.values() and c in RAW:
        return ("raw", db == 0, c)
    if db == 0:
        return ("A", da % 2, c if da != 2 else c % 2)
    return ("B", da, db % 2, c if db != 2 else c % 2)


def die_copies(order):
    copies, waiting, seen = [], {}, {}
    last = {}
    for i, item in enumerate(order):
        last[item if item[:2] == (0, 0) else group_of(*item)] = i
    at = [(last[e if e[:2] == (0, 0) else group_of(*e)], e) for e in order]
    for i, (da, db, c) in sorted(at, key=lambda v: v[0]):
        mat, off, rows = CHUNKS[c]
        held = waiting.setdefault((da, db, mat), [])
        held.append((off, rows))
        seen[da, db, mat] = seen.get((da, db, mat), 0) + rows
        if i >= len(order) - FINE_TAIL:
            copies += [(i, da, db, mat, *piece) for piece in held]
            held.clear()
        elif seen[da, db, mat] == ROWS:
            copies.append((i, da, db, mat, 0, ROWS))
            held.clear()
    return copies


ORDER = arrival_order()
DIE = die_copies(ORDER)
SENT_ROWS = sum(len(follow_ups(*item)) * CHUNKS[item[2]][2] for item in ORDER)
RAW_TOTAL = sum(CHUNKS[c][2] for c in RAW)


GROUPS = {}
for _item in ORDER:
    if _item[:2] != (0, 0):
        GROUPS.setdefault(group_of(*_item), []).append(_item)
GROUP_NUMBER = {g: i for i, g in enumerate(GROUPS)}


def gather_kernel(
    w_g, f_g, s_g, w_u, f_u, s_u, n_t, n_s,
    out_g, out_u, col_g, col_u, norm_out, latest_g, latest_u,
    first, second, part, pair, inverse, slots, nslots, n_in, raw,
    load_sem, send_sem, recv_sem, raw_send, die_send, die_recv,
    sum_send, sum_recv, n_send, n_recv,
):
    row = lax.axis_index("rows")
    x = lax.axis_index("cols")
    core = row % 2
    y = (row // 2) % 4
    z = row // 8
    a = y * (1 - core) + z * core
    b = z * (1 - core) + y * core
    stride_a = 2 + 6 * core
    stride_b = 8 - 6 * core
    partner = row + 1 - 2 * core
    outs = (out_g, out_u)
    latest = (latest_g, latest_u)

    def at_a(pos):
        return row + ((pos % 4) - a) * stride_a

    def at_b(pos):
        return row + ((pos % 4) - b) * stride_b

    def at_y(pos):
        return row + ((pos % 4) - y) * 2

    def at_z(pos):
        return row + ((pos % 4) - z) * 8

    half = ROWS // 2

    def first_of(m):
        return first.at[pl.ds(m * ROWS, ROWS)]

    for m, (w, f, s) in enumerate(((w_g, f_g, s_g), (w_u, f_u, s_u))):
        for h in range(2):
            at = pl.ds(h * half, half)
            for src, dst in ((w, latest[m]), (f, first_of(m)), (s, second.at[m])):
                copy = pltpu.make_async_copy(
                    src.at[at], dst.at[at], load_sem.at[2 * m + h]
                )
                copy.start()
    for j, src in enumerate((n_t, n_s)):
        pltpu.make_async_copy(src, n_in.at[j], load_sem.at[4]).start()

    barrier = pltpu.get_barrier_semaphore()
    peers = [(partner, x)]
    for d in range(1, 4):
        peers += [(at_y(y + d), x), (at_z(z + d), x), (row, (x + d) % 4)]
    for peer in peers:
        pl.semaphore_signal(barrier, inc=1, device_id=peer, device_id_type=MESH)

    for m in range(2):
        acc = jnp.zeros((8, WIDTH), jnp.float32)
        for h in range(2):
            three = first.at[pl.ds(0, 3 * half)]
            pltpu.make_async_copy(three, three, load_sem.at[2 * m + h]).wait()

            def step(i, acc, m=m):
                at = pl.ds(pl.multiple_of(i * 8, 8), 8)
                w = latest[m][at, :]
                new = w - learn_rate * (
                    first_of(m)[at, :] / (jnp.sqrt(second[m, at, :]) + tiny_value) + decay_rate * w
                )
                latest[m][at, :] = new
                return acc + jnp.abs(new)

            acc = lax.fori_loop(h * half // 8, (h + 1) * half // 8, step, acc)
        part[m] = jnp.sum(acc, axis=0, keepdims=True)

    pl.semaphore_wait(barrier, len(peers))

    def remote(src, dst, send, recv, device):
        return pltpu.make_async_remote_copy(
            src_ref=src, dst_ref=dst, send_sem=send, recv_sem=recv,
            device_id=device, device_id_type=MESH,
        )

    def start(src, dst, send, recv, device):
        remote(src, dst, send, recv, device).start()

    def arrived(ref, recv):
        remote(ref, ref, send_sem, recv, (partner, x)).wait_recv()

    def left(ref, send):
        remote(ref, ref, send, die_recv, (partner, x)).wait_send()

    links = {
        "A+": (at_a(a + 1), x), "A-": (at_a(a + 3), x),
        "B+": (at_b(b + 1), x), "B-": (at_b(b + 3), x),
    }
    raw_pieces = [(c, p) for c in RAW for p in range(0, CHUNKS[c][2], RAW_ROWS)]

    raw_row = {c: sum(CHUNKS[e][2] for e in RAW[:j]) for j, c in enumerate(RAW)}

    def send_raw(number):
        for _ in range(number):
            if not raw_pieces:
                return
            c, p = raw_pieces.pop(0)
            mat, off, _ = CHUNKS[c]
            for i, k in enumerate(LINKS):
                start(latest[mat].at[pl.ds(off + p, RAW_ROWS)],
                      raw.at[i, pl.ds(raw_row[c] + p, RAW_ROWS)], raw_send,
                      recv_sem.at[GROUP_NUMBER[group_of(*NEIGHBOURS[k], c)]], links[k])

    start(part, pair, sum_send, sum_recv.at[0], (partner, x))
    send_raw(RAW_BEFORE[0])

    def norm_stage(i, device_of, me):
        mine = nslots.at[4 * i + me]
        for d in range(1, 4):
            start(mine, mine, n_send, n_recv.at[i], device_of(d))

    def norm_wait(i):
        arrived(nslots.at[pl.ds(0, 3)], n_recv.at[i])
        total = nslots[4 * i]
        for k in range(1, 4):
            total = total + nslots[4 * i + k]
        return total

    pltpu.make_async_copy(n_in, n_in, load_sem.at[4]).wait()
    gain = n_in[0] + n_in[1]
    gain = jnp.broadcast_to(jnp.concatenate([gain] * 8, axis=1), (16, 128))
    place = lax.broadcasted_iota(jnp.int32, (16, 128), 0) * 8
    place = place + lax.broadcasted_iota(jnp.int32, (16, 128), 1) // 16
    nslots[x] = jnp.where(place == row * 4 + x, gain, 0.0)

    arrived(pair, sum_recv.at[0])
    places = ((y, z), (z, y))
    movers = ((at_y, at_z), (at_z, at_y))
    for m in range(2):
        slots[4 * m + places[m][0]] = part[m] + pair[m]
    for stage in range(2):
        for d in range(1, 4):
            for m in range(2):
                me = places[m][stage]
                mine = slots.at[8 * stage + 4 * m + me]
                start(mine, mine, sum_send, sum_recv.at[1 + stage], (movers[m][stage](me + d), x))
        send_raw(RAW_BEFORE[1 + stage])
        arrived(slots.at[pl.ds(0, 6)], sum_recv.at[1 + stage])
        for m in range(2):
            total = slots[8 * stage + 4 * m]
            for k in range(1, 4):
                total = total + slots[8 * stage + 4 * m + k]
            if stage == 0:
                slots[8 + 4 * m + places[m][1]] = total
            else:
                column = total * (1.0 / D_MODEL)
                (col_g, col_u)[m][...] = column
                inverse[m] = 1.0 / column
    norm_stage(0, lambda d: (row, (x + d) % 4), x)

    def block_row(da, db):
        return row + ((a + da) % 4 - a) * stride_a + ((b + db) % 4 - b) * stride_b

    def rows_of(owner, mat, off, rows):
        return outs[mat].at[pl.ds(pl.multiple_of(owner * ROWS + off, 16), rows)]

    passed = [0]

    def pass_on(da, db, c):
        here = rows_of(block_row(da, db), *CHUNKS[c])
        for link in follow_ups(da, db, c):
            group = group_of(*seen_by_receiver(link, da, db), c)
            start(here, here, send_sem, recv_sem.at[GROUP_NUMBER[group]], links[link])

    def pass_over(i):
        while passed[0] < len(DIE) and DIE[passed[0]][0] == i:
            _, ea, eb, mat, off, rows = DIE[passed[0]]
            block = rows_of(block_row(ea, eb), mat, off, rows)
            start(block, block, die_send, die_recv, (partner, x))
            passed[0] += 1

    def scaled(value, mat):
        return (value * inverse[mat]).astype(jnp.bfloat16)

    def norm_step(s):
        if s == 3:
            arrived(nslots.at[13], n_recv.at[3])
            norm_out[...] = (nslots[12] + nslots[13]).astype(jnp.bfloat16)
            return
        total = norm_wait(s)
        if s == 0:
            nslots[4 + y] = total
            norm_stage(1, lambda d: (at_y(y + d), x), y)
        elif s == 1:
            nslots[8 + z] = total
            norm_stage(2, lambda d: (at_z(z + d), x), z)
        else:
            nslots[12] = total
            start(nslots.at[12], nslots.at[13], n_send, n_recv.at[3], (partner, x))

    waiting = {g: list(members) for g, members in GROUPS.items()}
    norm_at = [NORM_FIRST + NORM_EVERY * k for k in range(4)]
    for i, (da, db, c) in enumerate(ORDER):
        if i in norm_at:
            norm_step(norm_at.index(i))
        mat, off, rows = CHUNKS[c]
        if (da, db) == (0, 0):
            for p in range(0, rows, 16):
                at = pl.ds(pl.multiple_of(row * ROWS + off + p, 16), 16)
                outs[mat][at, :] = scaled(latest[mat][off + p : off + p + 16, :], mat)
            pass_on(da, db, c)
            pass_over(i)
            continue
        group = group_of(da, db, c)
        waiting[group].remove((da, db, c))
        if waiting[group]:
            continue
        total = sum(CHUNKS[e][2] for _, _, e in GROUPS[group])
        if group[0] == "raw":
            arrived(first.at[pl.ds(0, total)], recv_sem.at[GROUP_NUMBER[group]])
        else:
            arrived(outs[0].at[pl.ds(0, total)], recv_sem.at[GROUP_NUMBER[group]])
        for ea, eb, e in GROUPS[group]:
            mat, off, rows = CHUNKS[e]
            if group[0] == "raw":
                k = list(NEIGHBOURS.values()).index((ea, eb))
                for p in range(0, rows, 16):
                    at = pl.ds(pl.multiple_of(block_row(ea, eb) * ROWS + off + p, 16), 16)
                    outs[mat][at, :] = scaled(raw[k, raw_row[e] + p : raw_row[e] + p + 16, :], mat)
            pass_on(ea, eb, e)
        pass_over(i)

    arrived(outs[0], die_recv)
    left(outs[0], die_send)
    left(outs[0].at[pl.ds(0, SENT_ROWS)], send_sem)
    left(first.at[pl.ds(0, 4 * RAW_TOTAL)], raw_send)
    left(slots.at[pl.ds(0, 14)], sum_send)
    left(nslots.at[pl.ds(0, 10)], n_send)


NORM_FIRST, NORM_EVERY = 12, 10
RAW_BEFORE = (1, 2, 1)


def gather(*args):
    f32, bf16 = jnp.float32, jnp.bfloat16
    dma = pltpu.SemaphoreType.DMA
    anywhere = pl.BlockSpec(memory_space=pl.ANY)
    on_chip = pl.BlockSpec(memory_space=pltpu.VMEM)
    return pl.pallas_call(
        gather_kernel,
        name="gather_kernel",
        out_shape=[
            pltpu.VMEM((D_MODEL, WIDTH), bf16),
            pltpu.VMEM((D_MODEL, WIDTH), bf16),
            pltpu.VMEM((1, WIDTH), f32),
            pltpu.VMEM((1, WIDTH), f32),
            pltpu.VMEM((16, 128), bf16),
            pltpu.VMEM((ROWS, WIDTH), f32),
            pltpu.VMEM((ROWS, WIDTH), f32),
        ],
        in_specs=[anywhere] * 8,
        out_specs=[on_chip] * 7,
        scratch_shapes=[
            pltpu.VMEM((2 * ROWS, WIDTH), f32),
            pltpu.VMEM((2, ROWS, WIDTH), f32),
            pltpu.VMEM((2, 1, WIDTH), f32),
            pltpu.VMEM((2, 1, WIDTH), f32),
            pltpu.VMEM((2, 1, WIDTH), f32),
            pltpu.VMEM((16, 1, WIDTH), f32),
            pltpu.VMEM((16, 16, 128), f32),
            pltpu.VMEM((2, 1, 16), f32),
            pltpu.VMEM((4, RAW_TOTAL, WIDTH), f32),
            dma((5,)),
            dma,
            dma((len(GROUPS),)),
            dma,
            dma,
            dma,
            dma,
            dma((3,)),
            dma,
            dma((4,)),
        ],
        compiler_params=pltpu.CompilerParams(
            collective_id=0, has_side_effects=True, vmem_limit_bytes=30 * 1024 * 1024
        ),
    )(*(pltpu.with_memory_space_constraint(v, pltpu.HBM) for v in args))


def write_kernel(*refs):
    k = len(refs) // 2
    srcs, dsts, sem = refs[:k], refs[k : 2 * k], refs[2 * k]
    copies, count = [], 0
    for src, dst in zip(srcs, dsts):
        pieces = WRITE_PIECES if src.shape[0] == D_MODEL else 1
        rows = src.shape[0] // pieces
        for p in range(pieces):
            at = pl.ds(p * rows, rows)
            copies.append(pltpu.make_async_copy(src.at[at], dst.at[at], sem.at[count]))
            count += 1
    for copy in copies:
        copy.start()
    for copy in copies:
        copy.wait()


WRITE_PIECES = 4


def write(arrays):
    anywhere = pl.BlockSpec(memory_space=pl.ANY)
    return pl.pallas_call(
        write_kernel,
        name="write_kernel",
        out_shape=[jax.ShapeDtypeStruct(v.shape, v.dtype) for v in arrays],
        in_specs=[anywhere] * len(arrays),
        out_specs=[anywhere] * len(arrays),
        scratch_shapes=[pltpu.SemaphoreType.DMA((2 * WRITE_PIECES + 5,))],
        compiler_params=pltpu.CompilerParams(vmem_limit_bytes=1024 * 1024),
    )(*arrays)


def local(w_gate, first_gate, second_gate, w_up, first_up, second_up, norm_train, norm_step):
    norms = (norm_train.reshape(1, 16), norm_step.reshape(1, 16))
    held = gather(w_gate, first_gate, second_gate, w_up, first_up, second_up, *norms)
    ready_g, ready_u, col_g, col_u, norm, latest_g, latest_u = write(held)
    return (
        ready_g,
        ready_u,
        col_g.reshape(WIDTH),
        col_u.reshape(WIDTH),
        norm.reshape(D_MODEL),
        latest_g,
        latest_u,
    )


def solution(mesh):
    split = P("rows", "cols")
    return jax.shard_map(
        local,
        mesh=mesh,
        in_specs=(split,) * 6 + (P(("rows", "cols")),) * 2,
        out_specs=(P(None, "cols"),) * 2 + (P("cols"),) * 2 + (P(),) + (split,) * 2,
        check_vma=False,
    )
```

time: 71 us -> 66.3 us (0.934)
  Pallas kernels: 69.3 us -> 65.6 us
  other arithmetic: 0.76 us -> 0 us
    pallas_call x1, Pallas kernels: 63.1 us -> 59.3 us  [gather(): pl.pallas_call(gather_kernel, name='gather_kernel', out_shape=[pltpu.VMEM...]
where the time goes in v2:
time: 66.3 us; the launch traced here: 66.2 us
  Pallas kernels  65.6 us (99%)
    pallas_call x1, Pallas kernels, gather(): pl.pallas_call(gather_kernel, name='gather_kernel', out_shape=[pltpu.VMEM...  59.3 us
    pallas_call x1, Pallas kernels, write(): pl.pallas_call(write_kernel, name='write_kernel', out_shape=[jax.ShapeDty...  6.25 us

profile of v2, /device:TPU:1, one launch (start us, length us, event | category | flops | bytes accessed | tf_op | source)
XLA Modules:
  0.0 66.2 jit_solution(13927732087935182073)
XLA Ops:
  0.6 59.3 %gather_kernel.1 = (bf16[2048,2048]{1,0:T(8,128)(2,1)S(1)}, bf16[2048,2048]{1,0:T(8,128)(2,1)S(1)}, f32[1,2048]{1,0:T(1,128)S(1)}, f32[1,2048]{1,0:T(1,128)S(1)}...) custom-call(f32[64,2048]{1,0:T(8,128)} %w_g.1, f32[64,2048]{1,0:T(8,128)} %f_g.1, ...), custom_call_target="tpu_custom_call" | custom-call | tf_op jit(solution)/shard_map/gather_kernel/pallas_call | solution.py:375
  60.0 6.2 %write_kernel.1 = (bf16[2048,2048]{1,0:T(8,128)(2,1)}, bf16[2048,2048]{1,0:T(8,128)(2,1)}, f32[1,2048]{1,0:T(1,128)}, f32[1,2048]{1,0:T(1,128)}, bf16[16,128]{1,...) custom-call(bf16[2048,2048]{1,0:T(8,128)(2,1)S(1)} %get-tuple-element.21.refs_0_, ...), custom_call_target="tpu_custom_call" | custom-call | tf_op jit(solution)/shard_map/write_kernel/pallas_call | solution.py:438

commit v3 on v2

--- a/solution.py
+++ b/solution.py
@@ -130,7 +130,7 @@
 def gather_kernel(
     w_g, f_g, s_g, w_u, f_u, s_u, n_t, n_s,
     out_g, out_u, col_g, col_u, norm_out, latest_g, latest_u,
-    first, second, part, pair, inverse, slots, nslots, n_in, raw,
+    first, second, inverse, slots, nslots, n_in, raw,
     load_sem, send_sem, recv_sem, raw_send, die_send, die_recv,
     sum_send, sum_recv, n_send, n_recv,
 ):
@@ -159,6 +159,9 @@
     def at_z(pos):
         return row + ((pos % 4) - z) * 8
 
+    places = ((y, z), (z, y))
+    movers = ((at_y, at_z), (at_z, at_y))
+
     half = ROWS // 2
 
     def first_of(m):
@@ -179,6 +182,7 @@
     peers = [(partner, x)]
     for d in range(1, 4):
         peers += [(at_y(y + d), x), (at_z(z + d), x), (row, (x + d) % 4)]
+        peers += [(at_y(y + d) + partner - row, x), (at_z(z + d) + partner - row, x)]
     for peer in peers:
         pl.semaphore_signal(barrier, inc=1, device_id=peer, device_id_type=MESH)
 
@@ -197,8 +201,8 @@
                 latest[m][at, :] = new
                 return acc + jnp.abs(new)
 
-            acc = lax.fori_loop(h * half // 8, (h + 1) * half // 8, step, acc)
-        part[m] = jnp.sum(acc, axis=0, keepdims=True)
+            acc = lax.fori_loop(h * half // 8, (h + 1) * half // 8, step, acc, unroll=True)
+        slots[8 * m + 2 * places[m][0] + core] = jnp.sum(acc, axis=0, keepdims=True)
 
     pl.semaphore_wait(barrier, len(peers))
 
@@ -236,7 +240,13 @@
                       raw.at[i, pl.ds(raw_row[c] + p, RAW_ROWS)], raw_send,
                       recv_sem.at[GROUP_NUMBER[group_of(*NEIGHBOURS[k], c)]], links[k])
 
-    start(part, pair, sum_send, sum_recv.at[0], (partner, x))
+    for d in (2, 1, 3, 0):
+        for m in range(2):
+            mine = slots.at[8 * m + 2 * places[m][0] + core]
+            there = movers[m][0](places[m][0] + d)
+            start(mine, mine, sum_send, sum_recv.at[0], (there + partner - row, x))
+            if d:
+                start(mine, mine, sum_send, sum_recv.at[0], (there, x))
     send_raw(RAW_BEFORE[0])
 
     def norm_stage(i, device_of, me):
@@ -258,27 +268,23 @@
     place = place + lax.broadcasted_iota(jnp.int32, (16, 128), 1) // 16
     nslots[x] = jnp.where(place == row * 4 + x, gain, 0.0)
 
-    arrived(pair, sum_recv.at[0])
-    places = ((y, z), (z, y))
-    movers = ((at_y, at_z), (at_z, at_y))
-    for m in range(2):
-        slots[4 * m + places[m][0]] = part[m] + pair[m]
-    for stage in range(2):
-        for d in range(1, 4):
-            for m in range(2):
-                me = places[m][stage]
-                mine = slots.at[8 * stage + 4 * m + me]
-                start(mine, mine, sum_send, sum_recv.at[1 + stage], (movers[m][stage](me + d), x))
-        send_raw(RAW_BEFORE[1 + stage])
-        arrived(slots.at[pl.ds(0, 6)], sum_recv.at[1 + stage])
+    for stage, count in enumerate((8, 4)):
+        if stage == 1:
+            for d in (2, 1, 3):
+                for m in range(2):
+                    mine = slots.at[16 + 4 * m + places[m][1]]
+                    start(mine, mine, sum_send, sum_recv.at[1],
+                          (movers[m][1](places[m][1] + d), x))
+            send_raw(RAW_BEFORE[1])
+        arrived(slots.at[pl.ds(0, (14, 6)[stage])], sum_recv.at[stage])
         for m in range(2):
-            total = slots[8 * stage + 4 * m]
-            for k in range(1, 4):
-                total = total + slots[8 * stage + 4 * m + k]
+            terms = [slots[16 * stage + count * m + k] for k in range(count)]
+            while len(terms) > 1:
+                terms = [p + q for p, q in zip(terms[::2], terms[1::2])]
             if stage == 0:
-                slots[8 + 4 * m + places[m][1]] = total
+                slots[16 + 4 * m + places[m][1]] = terms[0]
             else:
-                column = total * (1.0 / D_MODEL)
+                column = terms[0] * (1.0 / D_MODEL)
                 (col_g, col_u)[m][...] = column
                 inverse[m] = 1.0 / column
     norm_stage(0, lambda d: (row, (x + d) % 4), x)
@@ -358,13 +364,13 @@
     arrived(outs[0], die_recv)
     left(outs[0], die_send)
     left(outs[0].at[pl.ds(0, SENT_ROWS)], send_sem)
-    left(first.at[pl.ds(0, 4 * RAW_TOTAL)], raw_send)
-    left(slots.at[pl.ds(0, 14)], sum_send)
+    left(raw, raw_send)
+    left(slots.at[pl.ds(0, 20)], sum_send)
     left(nslots.at[pl.ds(0, 10)], n_send)
 
 
 NORM_FIRST, NORM_EVERY = 12, 10
-RAW_BEFORE = (1, 2, 1)
+RAW_BEFORE = (2, 2)
 
 
 def gather(*args):
@@ -390,9 +396,7 @@
             pltpu.VMEM((2 * ROWS, WIDTH), f32),
             pltpu.VMEM((2, ROWS, WIDTH), f32),
             pltpu.VMEM((2, 1, WIDTH), f32),
-            pltpu.VMEM((2, 1, WIDTH), f32),
-            pltpu.VMEM((2, 1, WIDTH), f32),
-            pltpu.VMEM((16, 1, WIDTH), f32),
+            pltpu.VMEM((24, 1, WIDTH), f32),
             pltpu.VMEM((16, 16, 128), f32),
             pltpu.VMEM((2, 1, 16), f32),
             pltpu.VMEM((4, RAW_TOTAL, WIDTH), f32),
@@ -403,7 +407,7 @@
             dma,
             dma,
             dma,
-            dma((3,)),
+            dma((2,)),
             dma,
             dma((4,)),
         ],

time: 66.3 us -> 65.7 us (level)
  Pallas kernels: 65.6 us -> 64.9 us
where the time goes in v3:
time: 65.7 us; the launch traced here: 65.6 us
  Pallas kernels  64.9 us (99%)
    pallas_call x1, Pallas kernels, gather(): pl.pallas_call(gather_kernel, name='gather_kernel', out_shape=[pltpu.VMEM...  58.7 us
    pallas_call x1, Pallas kernels, write(): pl.pallas_call(write_kernel, name='write_kernel', out_shape=[jax.ShapeDty...  6.25 us

profile of v3, /device:TPU:1, one launch (start us, length us, event | category | flops | bytes accessed | tf_op | source)
XLA Modules:
  0.0 65.6 jit_solution(17407503841665256657)
XLA Ops:
  0.6 58.7 %gather_kernel.1 = (bf16[2048,2048]{1,0:T(8,128)(2,1)S(1)}, bf16[2048,2048]{1,0:T(8,128)(2,1)S(1)}, f32[1,2048]{1,0:T(1,128)S(1)}, f32[1,2048]{1,0:T(1,128)S(1)}...) custom-call(f32[64,2048]{1,0:T(8,128)} %w_g.1, f32[64,2048]{1,0:T(8,128)} %f_g.1, ...), custom_call_target="tpu_custom_call" | custom-call | tf_op jit(solution)/shard_map/gather_kernel/pallas_call | solution.py:381
  59.3 6.2 %write_kernel.1 = (bf16[2048,2048]{1,0:T(8,128)(2,1)}, bf16[2048,2048]{1,0:T(8,128)(2,1)}, f32[1,2048]{1,0:T(1,128)}, f32[1,2048]{1,0:T(1,128)}, bf16[16,128]{1,...) custom-call(bf16[2048,2048]{1,0:T(8,128)(2,1)S(1)} %get-tuple-element.21.refs_0_, ...), custom_call_target="tpu_custom_call" | custom-call | tf_op jit(solution)/shard_map/write_kernel/pallas_call | solution.py:442

commit v4 on v3

--- a/solution.py
+++ b/solution.py
@@ -17,20 +17,21 @@
 decay_rate = 0.1
 tiny_value = 1e-08
 
-CHUNKS = ((0, 0, 32), (1, 0, 32), (0, 32, 32), (1, 32, 32))
+CHUNKS = ((0, 0, 32), (1, 0, 16), (1, 16, 16), (0, 32, 32), (1, 32, 16), (1, 48, 16))
 N = len(CHUNKS)
-RAW = (0,)
-LOW = (0, 1)
-HIGH = (2, 3)
+LOW = (0, 1, 2)
+HIGH = (3, 4, 5)
+FAR = (0, 1, 2, 0, 1, 2)
 RAW_ROWS = 8
 LINKS = ("A+", "A-", "B+", "B-")
 NEIGHBOURS = {"A+": (3, 0), "A-": (1, 0), "B+": (0, 3), "B-": (0, 1)}
+RAW = {0: LINKS, 1: ("A+", "A-")}
 FINE_TAIL = 14
 
 
 def follow_ups(da, db, c):
     if (da, db) == (0, 0):
-        return () if c in RAW else LINKS
+        return tuple(k for k in LINKS if k not in RAW.get(c, ()))
     if db == 0:
         on = ("B+", "B-")
         if da == 3 and c in LOW:
@@ -54,9 +55,9 @@
     delay = 1.4
     queues = {k: [] for k in LINKS}
     done = {k: 0.0 for k in queues}
-    first = [(0, 0, c) for c in range(N) if c not in RAW]
-    first += [NEIGHBOURS[k] + (c,) for c in RAW for k in LINKS]
-    first += [(0, 0, c) for c in RAW]
+    first = sorted([(0, 0, c) for c in range(N)], key=lambda v: len(RAW.get(v[2], ())) == 4)
+    spot = len(first) - sum(len(k) == 4 for k in RAW.values())
+    first[spot:spot] = [NEIGHBOURS[k] + (c,) for c in RAW for k in RAW[c]]
     events = [(0.0, i, item) for i, item in enumerate(first)]
     order, now, serial = [], 0.0, len(first)
     while events or any(queues.values()):
@@ -87,11 +88,11 @@
 
 
 def group_of(da, db, c):
-    if (da, db) in NEIGHBOURS.values() and c in RAW:
+    if (da, db) in [NEIGHBOURS[k] for k in RAW.get(c, ())]:
         return ("raw", db == 0, c)
     if db == 0:
-        return ("A", da % 2, c if da != 2 else c % 2)
-    return ("B", da, db % 2, c if db != 2 else c % 2)
+        return ("A", da % 2, c if da != 2 else FAR[c])
+    return ("B", da, db % 2, c if db != 2 else FAR[c])
 
 
 def die_copies(order):
@@ -117,7 +118,7 @@
 ORDER = arrival_order()
 DIE = die_copies(ORDER)
 SENT_ROWS = sum(len(follow_ups(*item)) * CHUNKS[item[2]][2] for item in ORDER)
-RAW_TOTAL = sum(CHUNKS[c][2] for c in RAW)
+RAW_TOTAL = sum(CHUNKS[c][2] * len(RAW[c]) for c in RAW)
 
 
 GROUPS = {}
@@ -227,7 +228,11 @@
     }
     raw_pieces = [(c, p) for c in RAW for p in range(0, CHUNKS[c][2], RAW_ROWS)]
 
-    raw_row = {c: sum(CHUNKS[e][2] for e in RAW[:j]) for j, c in enumerate(RAW)}
+    raw_row, rows_so_far = {}, 0
+    for c in RAW:
+        for k in RAW[c]:
+            raw_row[NEIGHBOURS[k] + (c,)] = rows_so_far
+            rows_so_far += CHUNKS[c][2]
 
     def send_raw(number):
         for _ in range(number):
@@ -235,9 +240,9 @@
                 return
             c, p = raw_pieces.pop(0)
             mat, off, _ = CHUNKS[c]
-            for i, k in enumerate(LINKS):
+            for k in RAW[c]:
                 start(latest[mat].at[pl.ds(off + p, RAW_ROWS)],
-                      raw.at[i, pl.ds(raw_row[c] + p, RAW_ROWS)], raw_send,
+                      raw.at[pl.ds(raw_row[NEIGHBOURS[k] + (c,)] + p, RAW_ROWS)], raw_send,
                       recv_sem.at[GROUP_NUMBER[group_of(*NEIGHBOURS[k], c)]], links[k])
 
     for d in (2, 1, 3, 0):
@@ -354,10 +359,10 @@
         for ea, eb, e in GROUPS[group]:
             mat, off, rows = CHUNKS[e]
             if group[0] == "raw":
-                k = list(NEIGHBOURS.values()).index((ea, eb))
                 for p in range(0, rows, 16):
                     at = pl.ds(pl.multiple_of(block_row(ea, eb) * ROWS + off + p, 16), 16)
-                    outs[mat][at, :] = scaled(raw[k, raw_row[e] + p : raw_row[e] + p + 16, :], mat)
+                    r = raw_row[ea, eb, e] + p
+                    outs[mat][at, :] = scaled(raw[r : r + 16, :], mat)
             pass_on(ea, eb, e)
         pass_over(i)
 
@@ -370,7 +375,7 @@
 
 
 NORM_FIRST, NORM_EVERY = 12, 10
-RAW_BEFORE = (2, 2)
+RAW_BEFORE = (3, 3)
 
 
 def gather(*args):
@@ -399,7 +404,7 @@
             pltpu.VMEM((24, 1, WIDTH), f32),
             pltpu.VMEM((16, 16, 128), f32),
             pltpu.VMEM((2, 1, 16), f32),
-            pltpu.VMEM((4, RAW_TOTAL, WIDTH), f32),
+            pltpu.VMEM((RAW_TOTAL, WIDTH), f32),
             dma((5,)),
             dma,
             dma((len(GROUPS),)),

time: 65.7 us -> 65.2 us (level)
  no operation moved by 1% of the time
where the time goes in v4:
time: 65.2 us; the launch traced here: 65.1 us
  Pallas kernels  64.4 us (99%)
    pallas_call x1, Pallas kernels, gather(): pl.pallas_call(gather_kernel, name='gather_kernel', out_shape=[pltpu.VMEM...  58.2 us
    pallas_call x1, Pallas kernels, write(): pl.pallas_call(write_kernel, name='write_kernel', out_shape=[jax.ShapeDty...  6.25 us

profile of v4, /device:TPU:1, one launch (start us, length us, event | category | flops | bytes accessed | tf_op | source)
XLA Modules:
  0.0 65.1 jit_solution(2067564500692372974)
XLA Ops:
  0.6 58.2 %gather_kernel.1 = (bf16[2048,2048]{1,0:T(8,128)(2,1)S(1)}, bf16[2048,2048]{1,0:T(8,128)(2,1)S(1)}, f32[1,2048]{1,0:T(1,128)S(1)}, f32[1,2048]{1,0:T(1,128)S(1)}...) custom-call(f32[64,2048]{1,0:T(8,128)} %w_g.1, f32[64,2048]{1,0:T(8,128)} %f_g.1, ...), custom_call_target="tpu_custom_call" | custom-call | tf_op jit(solution)/shard_map/gather_kernel/pallas_call | solution.py:386
  58.8 6.2 %write_kernel.1 = (bf16[2048,2048]{1,0:T(8,128)(2,1)}, bf16[2048,2048]{1,0:T(8,128)(2,1)}, f32[1,2048]{1,0:T(1,128)}, f32[1,2048]{1,0:T(1,128)}, bf16[16,128]{1,...) custom-call(bf16[2048,2048]{1,0:T(8,128)(2,1)S(1)} %get-tuple-element.21.refs_0_, ...), custom_call_target="tpu_custom_call" | custom-call | tf_op jit(solution)/shard_map/write_kernel/pallas_call | solution.py:447

commit v5 on v4

--- a/solution.py
+++ b/solution.py
@@ -140,10 +140,10 @@
     core = row % 2
     y = (row // 2) % 4
     z = row // 8
-    a = y * (1 - core) + z * core
-    b = z * (1 - core) + y * core
-    stride_a = 2 + 6 * core
-    stride_b = 8 - 6 * core
+    a = y * core + z * (1 - core)
+    b = z * core + y * (1 - core)
+    stride_a = 8 - 6 * core
+    stride_b = 2 + 6 * core
     partner = row + 1 - 2 * core
     outs = (out_g, out_u)
     latest = (latest_g, latest_u)
@@ -439,7 +439,7 @@
         copy.wait()
 
 
-WRITE_PIECES = 4
+WRITE_PIECES = 2
 
 
 def write(arrays):

time: 65.2 us -> 65.1 us (level)
  no operation moved by 1% of the time
where the time goes in v5:
time: 65.1 us; the launch traced here: 65 us
  Pallas kernels  64.4 us (99%)
    pallas_call x1, Pallas kernels, gather(): pl.pallas_call(gather_kernel, name='gather_kernel', out_shape=[pltpu.VMEM...  58.1 us
    pallas_call x1, Pallas kernels, write(): pl.pallas_call(write_kernel, name='write_kernel', out_shape=[jax.ShapeDty...  6.21 us

profile of v5, /device:TPU:1, one launch (start us, length us, event | category | flops | bytes accessed | tf_op | source)
XLA Modules:
  0.0 65.0 jit_solution(6992916708708083529)
XLA Ops:
  0.6 58.1 %gather_kernel.1 = (bf16[2048,2048]{1,0:T(8,128)(2,1)S(1)}, bf16[2048,2048]{1,0:T(8,128)(2,1)S(1)}, f32[1,2048]{1,0:T(1,128)S(1)}, f32[1,2048]{1,0:T(1,128)S(1)}...) custom-call(f32[64,2048]{1,0:T(8,128)} %w_g.1, f32[64,2048]{1,0:T(8,128)} %f_g.1, ...), custom_call_target="tpu_custom_call" | custom-call | tf_op jit(solution)/shard_map/gather_kernel/pallas_call | solution.py:386
  58.8 6.2 %write_kernel.1 = (bf16[2048,2048]{1,0:T(8,128)(2,1)}, bf16[2048,2048]{1,0:T(8,128)(2,1)}, f32[1,2048]{1,0:T(1,128)}, f32[1,2048]{1,0:T(1,128)}, bf16[16,128]{1,...) custom-call(bf16[2048,2048]{1,0:T(8,128)(2,1)S(1)} %get-tuple-element.21.refs_0_, ...), custom_call_target="tpu_custom_call" | custom-call | tf_op jit(solution)/shard_map/write_kernel/pallas_call | solution.py:447
